TPU v7x, 32 devices: a whole 2x2x4 slice. The times are simulated.
32 devices in a mesh: rep: 2 (over y), gx: 8 (over z, x), gy: 2 (over core).
Axes of the slice: x: 2, y: 2, z: 4, core: 2. Of those that a mesh axis runs over, the one named last changes fastest.
Arguments:
- tokens: bfloat16 [768, 8192], P(('rep', 'gx'), 'gy'), parts along dimension 0, may hold values from -6 to 6
- segment_ids: int32 [768], P(('rep', 'gx')), parts along dimension 0, may hold values from 0 to 1, as said below
- gate_weight: bfloat16 [8192, 2, 13312], P(None, 'gy', 'gx'), may hold values from -0.0625 to 0.0625
- up_weight: bfloat16 [8192, 2, 13312], P(None, 'gy', 'gx'), may hold values from -0.0625 to 0.0625
- down_weight: bfloat16 [2, 13312, 8192], P('gy', None, 'gx'), may hold values from -0.0390625 to 0.0390625
Outputs:
- grouped: bfloat16 [768, 8192], P(('rep', 'gx'), 'gy'), parts along dimension 0
There are 2 independent parts, one for each index of `rep`. A program takes and returns all parts, laid end to end along the dimension named above; an argument that names none is the same for every part. Nothing has to cross between parts.
Inputs may be any that keep to these rules, and one draw needn't show every extreme that they name: `segment_ids`: exactly 320 entries are 0 and 64 entries are 1.
All inputs are finite; a program needn't handle non-finite values.
Results may differ from a plain program's by a relative error of at most 0.0049.
Values may be sent and summed in bfloat16 or wider, within the bound.
A program may use at most 128 MiB of HBM per device.

v0:
```python
import jax
import jax.numpy as jnp
from jax import lax
from jax.sharding import PartitionSpec as P

PREFILL = 320


def grouped_target(token_kinds):
    decode_flag = token_kinds.astype(jnp.int32)
    prefill_flag = 1 - decode_flag
    prefill_rank = jnp.cumsum(prefill_flag) - 1
    decode_rank = jnp.cumsum(decode_flag) - 1
    return jnp.where(decode_flag == 0, prefill_rank, PREFILL + decode_rank)


def local(tokens, segment_ids, gate_weight, up_weight, down_weight):
    half_rows, token_kinds = (
        lax.all_gather(tokens, "gx", axis=0, tiled=True),
        lax.all_gather(segment_ids, "gx", axis=0, tiled=True),
    )
    gathered = lax.all_gather(half_rows, "gy", axis=1, tiled=True)
    gate_local = gate_weight.reshape(gate_weight.shape[0], -1)
    up_local = up_weight.reshape(up_weight.shape[0], -1)
    down_local = down_weight.reshape(-1, down_weight.shape[2])
    target = grouped_target(token_kinds)
    gate_value = jnp.dot(gathered, gate_local, preferred_element_type=jnp.float32)
    up_value = jnp.dot(gathered, up_local, preferred_element_type=jnp.float32)
    hidden = (jax.nn.silu(gate_value) * up_value).astype(jnp.bfloat16)
    partial_value = jnp.dot(
        lax.all_gather(hidden, "gx", axis=1, tiled=True),
        down_local,
        preferred_element_type=jnp.float32,
    )
    placed = jnp.zeros_like(partial_value).at[target].set(partial_value)
    switched = lax.all_to_all(placed, "gx", split_axis=0, concat_axis=1, tiled=True)
    return lax.psum_scatter(switched, "gy", scatter_dimension=1, tiled=True).astype(jnp.bfloat16)


def solution(mesh):
    placed = (
        P(("rep", "gx"), "gy"),
        P(("rep", "gx")),
        P(None, "gy", "gx"),
        P(None, "gy", "gx"),
        P("gy", None, "gx"),
    )
    return jax.shard_map(
        local, mesh=mesh, in_specs=placed, out_specs=P(("rep", "gx"), "gy"), check_vma=False
    )
```

profile of v0, /device:TPU:0, one launch (start us, length us, event | category | flops | bytes accessed | tf_op | source)
XLA Modules:
  0.0 349.0 jit_solution(17059045087787069002)
XLA Ops:
  6.5 0.0 all-gather.4.cloned.1.call-start
  6.5 0.7 all-gather.4.cloned.1.call-update
  7.3 0.0 all-gather.6.cloned.1.call-start
  7.3 65.0 %all-gather.4.cloned.1.call-done = bf16[384,4096]{1,0:T(8,128)(2,1)} async-done(((bf16[48,4096]{1,0:T(8,128)(2,1)}), bf16[384,4096]{1,0:T(8,128)(2,1)}) %all-gather.4.cloned.1.call-update) | async-done | bytes 3145744 | tf_op jit(solution)/shard_map/all_gather | solution.py:19
  72.3 0.0 all-gather.6.cloned.1.call-update
  72.3 0.0 all-gather.8.cloned.1.call-start
  72.4 16.9 %all-gather.6.cloned.1.call-done = bf16[384,8192]{1,0:T(8,128)(2,1)} async-done(((bf16[384,4096]{1,0:T(8,128)(2,1)}), bf16[384,8192]{1,0:T(8,128)(2,1)}) %all-gather.6.cloned.1.call-update) | async-done | bytes 6291472 | tf_op jit(solution)/shard_map/all_gather | solution.py:22
  89.3 0.0 copy-start
  89.3 17.7 %fusion.4 = f32[384,1664]{1,0:T(8,128)S(1)} fusion(bf16[384,8192]{1,0:T(8,128)(2,1)} %all-gather.6.cloned.1.call-done, bf16[8192,1,1664]{2,0,1:T(8,128)(2,1)} %param.7), kind=kOutput, calls=%fused_computation.5 | convolution fusion | flops 10468982784 | bytes 36110336 | tf_op jit(solution)/shard_map/dot_general | solution.py:27
  107.0 0.0 copy-done
  107.0 0.0 copy-start.2
  107.0 0.0 copy-start.1
  107.0 16.7 %fusion.9 = bf16[384,1664]{1,0:T(8,128)(2,1)} fusion(bf16[384,8192]{1,0:T(8,128)(2,1)S(1)} %copy-done, bf16[8192,1,1664]{2,0,1:T(8,128)(2,1)} %param.8, f32[384,1664]{1,0:T(8,128)S(1)} %fusion.4), kind=kOutput, calls=%fused_computation.8 | convolution fusion | flops 10472816640 | bytes 37388288 | tf_op jit(solution)/shard_map/dot_general | solution.py:28
  123.7 0.0 all-gather.8.cloned.1.call-update
  123.7 0.0 reduce-scatter.2.cloned.1.call-start
  123.8 0.0 copy-done.2
  123.8 0.6 dynamic-slice
  125.0 0.0 copy-done.1
  125.0 0.2 dynamic-update-slice
  125.3 11.6 %all-reduce = s32[384]{0:T(512)S(1)} all-reduce(s32[384]{0:T(512)S(1)} %dynamic-update-slice), channel_id=1, replica_groups=mesh['rep'=2,'gx'=8,'gy'=2] {'gx'}, use_global_device_ids=true, to_apply=%add | all-reduce | flops 384 | bytes 3072
  136.9 0.3 reduce-window.24
  137.2 0.1 slice.16
  137.3 0.3 reduce-window.16
  137.6 0.1 slice.14
  137.8 0.1 slice_reduce_fusion
  137.9 0.1 compare_select_fusion
  138.0 134.0 %all-gather.8.cloned.1.call-done = bf16[384,13312]{1,0:T(8,128)(2,1)} async-done(((bf16[384,1664]{1,0:T(8,128)(2,1)}), bf16[384,13312]{1,0:T(8,128)(2,1)}) %all-gather.8.cloned.1.call-update) | async-done | bytes 10223632 | tf_op jit(solution)/shard_map/all_gather | solution.py:31
  272.0 17.4 %fusion = f32[384,1024]{1,0:T(8,128)S(1)} fusion(bf16[384,13312]{1,0:T(8,128)(2,1)} %all-gather.8.cloned.1.call-done, bf16[1,13312,1024]{2,1,0:T(8,128)(2,1)} %param.9), kind=kOutput, calls=%fused_computation.1 | convolution fusion | flops 10468982784 | bytes 39059456 | tf_op jit(solution)/shard_map/dot_general | solution.py:30
  289.4 2.2 scatter_custom_fusion
  291.6 39.6 %all_to_all.19 = f32[8,48,1024]{2,1,0:T(8,128)S(1)} all-to-all(f32[8,48,1024]{2,1,0:T(8,128)S(1)} %bitcast.32), channel_id=1, replica_groups=mesh['rep'=2,'gx'=8,'gy'=2] {'gx'}, dimensions={0} | all-to-all | bytes 3145728 | tf_op jit(solution)/shard_map/all_to_all | solution.py:36
  331.2 1.3 copy.7
  332.4 0.0 reduce-scatter.2.cloned.1.call-update
  332.4 8.1 %reduce-scatter.2.cloned.1.call-done = f32[48,4096]{1,0:T(8,128)} async-done(((f32[48,8192]{1,0:T(8,128)}), f32[48,4096]{1,0:T(8,128)}) %reduce-scatter.2.cloned.1.call-update) | async-done | bytes 786448 | tf_op jit(solution)/shard_map/reduce_scatter | solution.py:37
  340.5 1.9 convert_element_type.7
  (4 shorter events, 0.1 us)
Async XLA Ops:
  6.5 65.7 %all-gather.4.cloned.1.call-start = ((), (), s32[]{:S(2)}) async-start(), calls=%async_computation.2 | async-start | bytes 3538944 | tf_op jit(solution)/shard_map/all_gather | solution.py:19
  7.3 82.0 %all-gather.6.cloned.1.call-start = ((), (), s32[]{:S(2)}) async-start(), calls=%async_computation.3 | async-start | bytes 9437184 | tf_op jit(solution)/shard_map/all_gather | solution.py:22
  72.3 199.7 %all-gather.8.cloned.1.call-start = ((), (), s32[]{:S(2)}) async-start(), calls=%async_computation.4 | async-start | bytes 11501568 | tf_op jit(solution)/shard_map/all_gather | solution.py:31
  89.3 17.7 %copy-start = (bf16[384,8192]{1,0:T(8,128)(2,1)S(1)}, bf16[384,8192]{1,0:T(8,128)(2,1)}, u32[]{:S(2)}) copy-start(bf16[384,8192]{1,0:T(8,128)(2,1)} %all-gather.6.cloned.1.call-done) | copy-start | bytes 18874372
  107.0 16.8 %copy-start.2 = (u32[32]{0:T(128)S(1)}, u32[32]{0:T(128)}, u32[]{:S(2)}) copy-start(u32[32]{0:T(128)} %constant.26) | copy-start | bytes 388
  107.0 18.0 %copy-start.1 = (s32[48]{0:T(128)S(1)}, s32[48]{0:T(128)}, u32[]{:S(2)}) copy-start(s32[48]{0:T(128)} %param.6) | copy-start | bytes 580
  123.7 216.8 %reduce-scatter.2.cloned.1.call-start = ((), (), s32[]{:S(2)}) async-start(), calls=%async_computation.5 | async-start | bytes 2359296 | tf_op jit(solution)/shard_map/reduce_scatter | solution.py:37
Sparse Core Ops, SparseCore 0:
  9.5 62.7 all-gather.3
  73.8 15.4 all-gather.5
  123.8 148.1 all-gather.7
  332.6 7.9 reduce-scatter.1
where the time goes:
time: 349 us
  waiting for transfers between devices  225 us (64%)
  matrix products  51.7 us (15%)
  blocking collectives  51.2 us (15%)
  between operations  13.9 us (4%)
  local copies, waits for them, and re-layouts  4.61 us (1%)
    all_gather x1, waiting for transfers between devices, local(): lax.all_gather(hidden, 'gx', axis=1, tiled=True)  134 us
    all_gather x1, waiting for transfers between devices, local(): lax.all_gather(tokens, 'gx', axis=0, tiled=True)  65 us
    all_to_all x1, blocking collectives, local(): lax.all_to_all(placed, 'gx', split_axis=0, concat_axis=1, tiled=True)  39.6 us
    dot_general x1, matrix products, local(): jnp.dot(gathered, gate_local, preferred_element_type=jnp.float32)  17.7 us
    dot_general x1, matrix products, local(): jnp.dot(lax.all_gather(hidden, 'gx', axis=1, tiled=True), down_local, pre...  17.4 us
    all_gather x1, waiting for transfers between devices, local(): gathered = lax.all_gather(half_rows, 'gy', axis=1, tiled=True)  16.9 us
    dot_general x1, matrix products, local(): up_value = jnp.dot(gathered, up_local, preferred_element_type=jnp.float32)  16.7 us
    unnamed x1, blocking collectives  11.6 us
  transfers between devices with their start and end apart: 4, of which 4 were waited for; matrix products, arithmetic and copies ran while one was open for 1% of the time, Pallas kernels for 0%

commit v1 on v0

--- a/solution.py
+++ b/solution.py
@@ -4,6 +4,13 @@
 from jax.sharding import PartitionSpec as P
 
 PREFILL = 320
+
+
+def all_by_exchange(array, axis, d):
+    size = lax.axis_size(axis)
+    shards = jnp.stack([array for _ in range(size)])
+    shards = lax.all_to_all(shards, axis, split_axis=0, concat_axis=0)
+    return jnp.concatenate(shards, axis=d)
 
 
 def grouped_target(token_kinds):
@@ -16,7 +23,7 @@
 
 def local(tokens, segment_ids, gate_weight, up_weight, down_weight):
     half_rows, token_kinds = (
-        lax.all_gather(tokens, "gx", axis=0, tiled=True),
+        all_by_exchange(tokens, "gx", 0),
         lax.all_gather(segment_ids, "gx", axis=0, tiled=True),
     )
     gathered = lax.all_gather(half_rows, "gy", axis=1, tiled=True)

time: 349 us -> 362 us (1.037)
  blocking collectives: 51.2 us -> 129 us
  waiting for transfers between devices: 225 us -> 158 us
    all_to_all x0 -> x1, blocking collectives: none -> 77.9 us  [all_by_exchange(): shards = lax.all_to_all(shards, axis, split_axis=0, concat_axis=0)]
    all_gather x1 -> x0, waiting for transfers between devices: 65 us -> none  [local(): lax.all_gather(tokens, 'gx', axis=0, tiled=True)]
  transfers between devices with their start and end apart: 4 -> 3, of which waited for: 4 -> 3; matrix products, arithmetic and copies ran while one was open for 1% -> 1% of each run, Pallas kernels for 0% -> 0%
where the time goes in v1:
time: 362 us; the launch traced here: 361 us
  waiting for transfers between devices  158 us (44%)
  blocking collectives  129 us (36%)
  matrix products  51.7 us (14%)
  between operations  13.9 us (4%)
  local copies, waits for them, and re-layouts  5.97 us (2%)
    all_gather x1, waiting for transfers between devices, local(): lax.all_gather(hidden, 'gx', axis=1, tiled=True)  134 us
    all_to_all x1, blocking collectives, all_by_exchange(): shards = lax.all_to_all(shards, axis, split_axis=0, concat_axis=0)  77.9 us
    all_to_all x1, blocking collectives, local(): lax.all_to_all(placed, 'gx', split_axis=0, concat_axis=1, tiled=True)  39.6 us
    dot_general x1, matrix products, local(): jnp.dot(gathered, gate_local, preferred_element_type=jnp.float32)  17.7 us
    dot_general x1, matrix products, local(): jnp.dot(lax.all_gather(hidden, 'gx', axis=1, tiled=True), down_local, pre...  17.4 us
    dot_general x1, matrix products, local(): up_value = jnp.dot(gathered, up_local, preferred_element_type=jnp.float32)  16.7 us
    all_gather x1, waiting for transfers between devices, local(): gathered = lax.all_gather(half_rows, 'gy', axis=1, tiled=True)  15.9 us
    unnamed x1, blocking collectives  11.6 us
  transfers between devices with their start and end apart: 3, of which 3 were waited for; matrix products, arithmetic and copies ran while one was open for 1% of the time, Pallas kernels for 0%

profile of v1, /device:TPU:0, one launch (start us, length us, event | category | flops | bytes accessed | tf_op | source)
XLA Modules:
  0.0 361.5 jit_solution(18357568223474170661)
XLA Ops:
  6.5 0.0 all-gather.3.cloned.1.call-start
  6.5 1.4 stack.2
  7.9 77.9 %all_to_all.24 = bf16[8,48,4096]{2,1,0:T(8,128)(2,1)} all-to-all(bf16[8,48,4096]{2,1,0:T(8,128)(2,1)S(1)} %stack.2), channel_id=1, replica_groups=mesh['rep'=2,'gx'=8,'gy'=2] {'gx'}, dimensions={0} | all-to-all | bytes 6291456 | tf_op jit(solution)/shard_map/all_to_all | solution.py:12
  85.8 0.0 all-gather.3.cloned.1.call-update
  85.8 0.0 all-gather.5.cloned.1.call-start
  85.9 15.9 %all-gather.3.cloned.1.call-done = bf16[384,8192]{1,0:T(8,128)(2,1)} async-done(((bf16[384,4096]{1,0:T(8,128)(2,1)}), bf16[384,8192]{1,0:T(8,128)(2,1)}) %all-gather.3.cloned.1.call-update) | async-done | bytes 6291472 | tf_op jit(solution)/shard_map/all_gather | solution.py:29
  101.8 0.0 copy-start
  101.8 17.7 %fusion.4 = f32[384,1664]{1,0:T(8,128)S(1)} fusion(bf16[384,8192]{1,0:T(8,128)(2,1)} %all-gather.3.cloned.1.call-done, bf16[8192,1,1664]{2,0,1:T(8,128)(2,1)} %param.7), kind=kOutput, calls=%fused_computation.5 | convolution fusion | flops 10468982784 | bytes 36110336 | tf_op jit(solution)/shard_map/dot_general | solution.py:34
  119.4 0.0 copy-done
  119.5 0.0 copy-start.2
  119.5 0.0 copy-start.1
  119.5 16.7 %fusion.9 = bf16[384,1664]{1,0:T(8,128)(2,1)} fusion(bf16[384,8192]{1,0:T(8,128)(2,1)S(1)} %copy-done, bf16[8192,1,1664]{2,0,1:T(8,128)(2,1)} %param.8, f32[384,1664]{1,0:T(8,128)S(1)} %fusion.4), kind=kOutput, calls=%fused_computation.8 | convolution fusion | flops 10472816640 | bytes 37388288 | tf_op jit(solution)/shard_map/dot_general | solution.py:35
  136.2 0.0 all-gather.5.cloned.1.call-update
  136.2 0.0 reduce-scatter.2.cloned.1.call-start
  136.2 0.0 copy-done.2
  136.3 0.6 dynamic-slice
  137.5 0.0 copy-done.1
  137.5 0.2 dynamic-update-slice
  137.8 11.6 %all-reduce = s32[384]{0:T(512)S(1)} all-reduce(s32[384]{0:T(512)S(1)} %dynamic-update-slice), channel_id=1, replica_groups=mesh['rep'=2,'gx'=8,'gy'=2] {'gx'}, use_global_device_ids=true, to_apply=%add | all-reduce | flops 384 | bytes 3072
  149.4 0.3 reduce-window.24
  149.7 0.1 slice.16
  149.8 0.3 reduce-window.16
  150.1 0.1 slice.14
  150.2 0.1 slice_reduce_fusion
  150.4 0.1 compare_select_fusion
  150.5 134.0 %all-gather.5.cloned.1.call-done = bf16[384,13312]{1,0:T(8,128)(2,1)} async-done(((bf16[384,1664]{1,0:T(8,128)(2,1)}), bf16[384,13312]{1,0:T(8,128)(2,1)}) %all-gather.5.cloned.1.call-update) | async-done | bytes 10223632 | tf_op jit(solution)/shard_map/all_gather | solution.py:38
  284.5 17.4 %fusion = f32[384,1024]{1,0:T(8,128)S(1)} fusion(bf16[384,13312]{1,0:T(8,128)(2,1)} %all-gather.5.cloned.1.call-done, bf16[1,13312,1024]{2,1,0:T(8,128)(2,1)} %param.9), kind=kOutput, calls=%fused_computation.1 | convolution fusion | flops 10468982784 | bytes 39059456 | tf_op jit(solution)/shard_map/dot_general | solution.py:37
  301.8 2.2 scatter_custom_fusion
  304.1 39.6 %all_to_all.25 = f32[8,48,1024]{2,1,0:T(8,128)S(1)} all-to-all(f32[8,48,1024]{2,1,0:T(8,128)S(1)} %bitcast.34), channel_id=1, replica_groups=mesh['rep'=2,'gx'=8,'gy'=2] {'gx'}, dimensions={0} | all-to-all | bytes 3145728 | tf_op jit(solution)/shard_map/all_to_all | solution.py:43
  343.6 1.3 copy.7
  344.9 0.0 reduce-scatter.2.cloned.1.call-update
  344.9 8.1 %reduce-scatter.2.cloned.1.call-done = f32[48,4096]{1,0:T(8,128)} async-done(((f32[48,8192]{1,0:T(8,128)}), f32[48,4096]{1,0:T(8,128)}) %reduce-scatter.2.cloned.1.call-update) | async-done | bytes 786448 | tf_op jit(solution)/shard_map/reduce_scatter | solution.py:44
  353.0 1.9 convert_element_type.7
  (4 shorter events, 0.1 us)
Async XLA Ops:
  6.5 95.2 %all-gather.3.cloned.1.call-start = ((), (), s32[]{:S(2)}) async-start(), calls=%async_computation.3 | async-start | bytes 9437184 | tf_op jit(solution)/shard_map/all_gather | solution.py:29
  85.8 198.6 %all-gather.5.cloned.1.call-start = ((), (), s32[]{:S(2)}) async-start(), calls=%async_computation.4 | async-start | bytes 11501568 | tf_op jit(solution)/shard_map/all_gather | solution.py:38
  101.8 17.7 %copy-start = (bf16[384,8192]{1,0:T(8,128)(2,1)S(1)}, bf16[384,8192]{1,0:T(8,128)(2,1)}, u32[]{:S(2)}) copy-start(bf16[384,8192]{1,0:T(8,128)(2,1)} %all-gather.3.cloned.1.call-done) | copy-start | bytes 18874372
  119.5 16.8 %copy-start.2 = (u32[32]{0:T(128)S(1)}, u32[32]{0:T(128)}, u32[]{:S(2)}) copy-start(u32[32]{0:T(128)} %constant.26) | copy-start | bytes 388
  119.5 18.0 %copy-start.1 = (s32[48]{0:T(128)S(1)}, s32[48]{0:T(128)}, u32[]{:S(2)}) copy-start(s32[48]{0:T(128)} %param.6) | copy-start | bytes 580
  136.2 216.8 %reduce-scatter.2.cloned.1.call-start = ((), (), s32[]{:S(2)}) async-start(), calls=%async_computation.5 | async-start | bytes 2359296 | tf_op jit(solution)/shard_map/reduce_scatter | solution.py:44
Sparse Core Ops, SparseCore 0:
  85.9 15.7 all-gather.2
  136.3 148.1 all-gather.4
  345.0 7.9 reduce-scatter.1

commit v2 on v0

--- a/solution.py
+++ b/solution.py
@@ -33,7 +33,10 @@
         preferred_element_type=jnp.float32,
     )
     placed = jnp.zeros_like(partial_value).at[target].set(partial_value)
-    switched = lax.all_to_all(placed, "gx", split_axis=0, concat_axis=1, tiled=True)
+    devices = lax.axis_size("gx")
+    blocks = jnp.stack(jnp.split(placed, devices, axis=0), axis=0)
+    blocks = lax.all_to_all(blocks, "gx", split_axis=0, concat_axis=0)
+    switched = jnp.concatenate(blocks, axis=1)
     return lax.psum_scatter(switched, "gy", scatter_dimension=1, tiled=True).astype(jnp.bfloat16)
 
 

time: 349 us -> 349 us (level)
  no operation moved by 1% of the time
where the time goes in v2:
time: 349 us
  waiting for transfers between devices  225 us (64%)
  matrix products  51.7 us (15%)
  blocking collectives  51.2 us (15%)
  between operations  13.9 us (4%)
  local copies, waits for them, and re-layouts  4.74 us (1%)
    all_gather x1, waiting for transfers between devices, local(): lax.all_gather(hidden, 'gx', axis=1, tiled=True)  134 us
    all_gather x1, waiting for transfers between devices, local(): lax.all_gather(tokens, 'gx', axis=0, tiled=True)  65 us
    all_to_all x1, blocking collectives, local(): blocks = lax.all_to_all(blocks, 'gx', split_axis=0, concat_axis=0)  39.6 us
    dot_general x1, matrix products, local(): jnp.dot(gathered, gate_local, preferred_element_type=jnp.float32)  17.7 us
    dot_general x1, matrix products, local(): jnp.dot(lax.all_gather(hidden, 'gx', axis=1, tiled=True), down_local, pre...  17.4 us
    all_gather x1, waiting for transfers between devices, local(): gathered = lax.all_gather(half_rows, 'gy', axis=1, tiled=True)  16.9 us
    dot_general x1, matrix products, local(): up_value = jnp.dot(gathered, up_local, preferred_element_type=jnp.float32)  16.7 us
    unnamed x1, blocking collectives  11.6 us
  transfers between devices with their start and end apart: 4, of which 4 were waited for; matrix products, arithmetic and copies ran while one was open for 1% of the time, Pallas kernels for 0%

profile of v2, /device:TPU:0, one launch (start us, length us, event | category | flops | bytes accessed | tf_op | source)
XLA Modules:
  0.0 349.2 jit_solution(16798101019915804254)
XLA Ops:
  6.5 0.0 all-gather.4.cloned.1.call-start
  6.5 0.7 all-gather.4.cloned.1.call-update
  7.3 0.0 all-gather.6.cloned.1.call-start
  7.3 65.0 %all-gather.4.cloned.1.call-done = bf16[384,4096]{1,0:T(8,128)(2,1)} async-done(((bf16[48,4096]{1,0:T(8,128)(2,1)}), bf16[384,4096]{1,0:T(8,128)(2,1)}) %all-gather.4.cloned.1.call-update) | async-done | bytes 3145744 | tf_op jit(solution)/shard_map/all_gather | solution.py:19
  72.3 0.0 all-gather.6.cloned.1.call-update
  72.3 0.0 all-gather.8.cloned.1.call-start
  72.4 16.9 %all-gather.6.cloned.1.call-done = bf16[384,8192]{1,0:T(8,128)(2,1)} async-done(((bf16[384,4096]{1,0:T(8,128)(2,1)}), bf16[384,8192]{1,0:T(8,128)(2,1)}) %all-gather.6.cloned.1.call-update) | async-done | bytes 6291472 | tf_op jit(solution)/shard_map/all_gather | solution.py:22
  89.3 0.0 copy-start
  89.3 17.7 %fusion.4 = f32[384,1664]{1,0:T(8,128)S(1)} fusion(bf16[384,8192]{1,0:T(8,128)(2,1)} %all-gather.6.cloned.1.call-done, bf16[8192,1,1664]{2,0,1:T(8,128)(2,1)} %param.7), kind=kOutput, calls=%fused_computation.5 | convolution fusion | flops 10468982784 | bytes 36110336 | tf_op jit(solution)/shard_map/dot_general | solution.py:27
  107.0 0.0 copy-done
  107.0 0.0 copy-start.2
  107.0 0.0 copy-start.1
  107.0 16.7 %fusion.9 = bf16[384,1664]{1,0:T(8,128)(2,1)} fusion(bf16[384,8192]{1,0:T(8,128)(2,1)S(1)} %copy-done, bf16[8192,1,1664]{2,0,1:T(8,128)(2,1)} %param.8, f32[384,1664]{1,0:T(8,128)S(1)} %fusion.4), kind=kOutput, calls=%fused_computation.8 | convolution fusion | flops 10472816640 | bytes 37388288 | tf_op jit(solution)/shard_map/dot_general | solution.py:28
  123.7 0.0 all-gather.8.cloned.1.call-update
  123.7 0.0 reduce-scatter.2.cloned.1.call-start
  123.8 0.0 copy-done.2
  123.8 0.6 dynamic-slice
  125.0 0.0 copy-done.1
  125.0 0.2 dynamic-update-slice
  125.3 11.6 %all-reduce = s32[384]{0:T(512)S(1)} all-reduce(s32[384]{0:T(512)S(1)} %dynamic-update-slice), channel_id=1, replica_groups=mesh['rep'=2,'gx'=8,'gy'=2] {'gx'}, use_global_device_ids=true, to_apply=%add | all-reduce | flops 384 | bytes 3072
  136.9 0.3 reduce-window.24
  137.2 0.1 slice.16
  137.3 0.3 reduce-window.16
  137.6 0.1 slice.14
  137.8 0.1 slice_reduce_fusion
  137.9 0.1 compare_select_fusion
  138.0 134.0 %all-gather.8.cloned.1.call-done = bf16[384,13312]{1,0:T(8,128)(2,1)} async-done(((bf16[384,1664]{1,0:T(8,128)(2,1)}), bf16[384,13312]{1,0:T(8,128)(2,1)}) %all-gather.8.cloned.1.call-update) | async-done | bytes 10223632 | tf_op jit(solution)/shard_map/all_gather | solution.py:31
  272.0 17.4 %fusion = f32[384,1024]{1,0:T(8,128)S(1)} fusion(bf16[384,13312]{1,0:T(8,128)(2,1)} %all-gather.8.cloned.1.call-done, bf16[1,13312,1024]{2,1,0:T(8,128)(2,1)} %param.9), kind=kOutput, calls=%fused_computation.1 | convolution fusion | flops 10468982784 | bytes 39059456 | tf_op jit(solution)/shard_map/dot_general | solution.py:30
  289.4 2.2 scatter_custom_fusion
  291.8 39.6 %all_to_all.5 = f32[8,48,1024]{2,1,0:T(8,128)S(1)} all-to-all(f32[8,48,1024]{2,1,0:T(8,128)S(1)} %fusion.14), channel_id=1, replica_groups=mesh['rep'=2,'gx'=8,'gy'=2] {'gx'}, dimensions={0} | all-to-all | bytes 3145728 | tf_op jit(solution)/shard_map/all_to_all | solution.py:38
  331.3 1.3 copy.21
  332.6 0.0 reduce-scatter.2.cloned.1.call-update
  332.6 8.1 %reduce-scatter.2.cloned.1.call-done = f32[48,4096]{1,0:T(8,128)} async-done(((f32[48,8192]{1,0:T(8,128)}), f32[48,4096]{1,0:T(8,128)}) %reduce-scatter.2.cloned.1.call-update) | async-done | bytes 786448 | tf_op jit(solution)/shard_map/reduce_scatter | solution.py:40
  340.7 1.9 convert_element_type.7
  (12 shorter events, 0.2 us)
Async XLA Ops:
  6.5 65.7 %all-gather.4.cloned.1.call-start = ((), (), s32[]{:S(2)}) async-start(), calls=%async_computation.2 | async-start | bytes 3538944 | tf_op jit(solution)/shard_map/all_gather | solution.py:19
  7.3 82.0 %all-gather.6.cloned.1.call-start = ((), (), s32[]{:S(2)}) async-start(), calls=%async_computation.3 | async-start | bytes 9437184 | tf_op jit(solution)/shard_map/all_gather | solution.py:22
  72.3 199.7 %all-gather.8.cloned.1.call-start = ((), (), s32[]{:S(2)}) async-start(), calls=%async_computation.4 | async-start | bytes 11501568 | tf_op jit(solution)/shard_map/all_gather | solution.py:31
  89.3 17.7 %copy-start = (bf16[384,8192]{1,0:T(8,128)(2,1)S(1)}, bf16[384,8192]{1,0:T(8,128)(2,1)}, u32[]{:S(2)}) copy-start(bf16[384,8192]{1,0:T(8,128)(2,1)} %all-gather.6.cloned.1.call-done) | copy-start | bytes 18874372
  107.0 16.8 %copy-start.2 = (u32[32]{0:T(128)S(1)}, u32[32]{0:T(128)}, u32[]{:S(2)}) copy-start(u32[32]{0:T(128)} %constant.26) | copy-start | bytes 388
  107.0 18.0 %copy-start.1 = (s32[48]{0:T(128)S(1)}, s32[48]{0:T(128)}, u32[]{:S(2)}) copy-start(s32[48]{0:T(128)} %param.6) | copy-start | bytes 580
  123.7 217.0 %reduce-scatter.2.cloned.1.call-start = ((), (), s32[]{:S(2)}) async-start(), calls=%async_computation.5 | async-start | bytes 2359296 | tf_op jit(solution)/shard_map/reduce_scatter | solution.py:40
Sparse Core Ops, SparseCore 0:
  9.5 62.7 all-gather.3
  73.8 15.4 all-gather.5
  123.8 148.1 all-gather.7
  332.7 7.9 reduce-scatter.1
